TPU v7x, 256 devices: a whole 4x4x8 slice. The times are simulated.
256 devices in a mesh: rows: 64 (over z, y, core), panel: 4 (over x).
Axes of the slice: x: 4, y: 4, z: 8, core: 2. Of those that a mesh axis runs over, the one named last changes fastest.
Arguments:
- pair_block: bfloat16 [2048, 16384], P('rows', 'panel'), may hold values from -6 to 6
- resolvent: float32 [16384, 16384], P('panel', 'rows'), may hold values from -0.046875 to 0.046875
- virt_coef: bfloat16 [1024, 11200], P('rows', 'panel'), may hold values from -0.1875 to 0.1875
- slot_row: int32 [2048], replicated, may hold values from 0 to 2047, each once
Outputs:
- backward: float32 [2, 11200, 16384], P(None, 'panel', 'rows')
Inputs may be any that keep to these rules, and one draw needn't show every extreme that they name: `slot_row`: every pair row appears exactly once.
All inputs are finite; a program needn't handle non-finite values.
Results may differ from a plain program's by a relative error of at most 0.0041.
Values may be sent and summed in bfloat16 or wider, within the bound.
A program may use at most 128 MiB of HBM per device.

v0:
```python
import jax
import jax.numpy as jnp
from jax import lax
from jax.sharding import PartitionSpec as P

OCC_B = 2


def body(pair_block, resolvent, virt_coef, slot_row):
    resolvent_round = resolvent.astype(jnp.bfloat16)
    gathered = None
    partial_sum = jnp.dot(
        lax.all_gather(pair_block, "rows", axis=0, tiled=True),
        resolvent_round,
        preferred_element_type=jnp.float32,
    )
    gathered = lax.psum(partial_sum, "panel").astype(jnp.bfloat16)
    grouped = jnp.take(gathered, slot_row, axis=0)
    grouped = grouped.reshape(OCC_B, slot_row.shape[0] // OCC_B, gathered.shape[1])
    coef_all = lax.all_gather(virt_coef, "rows", axis=0, tiled=True)
    return jnp.einsum("am,oac->omc", coef_all, grouped, preferred_element_type=jnp.float32)


def solution(mesh):
    placed = (P("rows", "panel"), P("panel", "rows"), P("rows", "panel"), P())
    return jax.shard_map(
        body, mesh=mesh, in_specs=placed, out_specs=P(None, "panel", "rows"), check_vma=False
    )
```

profile of v0, /device:TPU:1, one launch (start us, length us, event | category | flops | bytes accessed | tf_op | source)
XLA Modules:
  0.0 209.5 jit_solution(6740521300446435897)
XLA Ops:
  6.5 0.0 all-gather.3.cloned.1.call-start
  6.5 0.7 all-gather.3.cloned.1.call-update
  7.3 0.0 all-gather.5.cloned.1.call-start
  7.3 0.7 all-gather.5.cloned.1.call-update
  8.0 0.7 compare_and_fusion
  8.7 0.7 fusion.10
  9.4 104.2 %all-gather.3.cloned.1.call-done = bf16[2048,4096]{1,0:T(8,128)(2,1)} async-done(((bf16[32,4096]{1,0:T(8,128)(2,1)}), bf16[2048,4096]{1,0:T(8,128)(2,1)}) %all-gather.3.cloned.1.call-update) | async-done | bytes 16777232 | tf_op jit(solution)/shard_map/all_gather | solution.py:13
  113.6 9.3 %fusion.5 = f32[2048,256]{1,0:T(8,128)S(1)} fusion(bf16[2048,4096]{1,0:T(8,128)(2,1)} %all-gather.3.cloned.1.call-done, f32[4096,256]{1,0:T(8,128)} %param.5), kind=kOutput, calls=%fused_computation.4 | convolution fusion | flops 4296015872 | bytes 23068672 | tf_op jit(solution)/shard_map/dot_general | solution.py:12
  122.9 42.3 %all-reduce.1 = bf16[2048,256]{1,0:T(8,128)(2,1)S(1)} all-reduce(f32[2048,256]{1,0:T(8,128)S(1)} %fusion.5), channel_id=1, replica_groups=mesh['rows'=64,'panel'=4] {'panel'}, use_global_device_ids=true, to_apply=%region_0.0 | all-reduce | flops 524288 | bytes 3145728 | tf_op jit(solution)/shard_map/psum | solution.py:17
  165.2 7.5 %gather_fusion = bf16[2048,256]{1,0:T(8,128)(2,1)S(1)} fusion(bf16[2048,256]{1,0:T(8,128)(2,1)S(1)} %all-reduce.1, s32[2048]{0:T(1024)S(1)} %fusion.10), kind=kCustom, calls=%fused_computation | custom fusion | bytes 2105344 | tf_op jit(solution)/shard_map/jit(_take)/gather | solution.py:18
  172.7 20.7 %all-gather.5.cloned.1.call-done = bf16[1024,2800]{1,0:T(8,128)(2,1)} async-done(((bf16[16,2800]{1,0:T(8,128)(2,1)}), bf16[1024,2800]{1,0:T(8,128)(2,1)}) %all-gather.5.cloned.1.call-update) | async-done | bytes 5734416 | tf_op jit(solution)/shard_map/all_gather | solution.py:20
  193.4 9.2 %fusion.2 = f32[2,2800,256]{2,1,0:T(8,128)} fusion(bf16[1024,2800]{1,0:T(8,128)(2,1)} %all-gather.5.cloned.1.call-done, bf16[2,1024,256]{2,1,0:T(8,128)(2,1)S(1)} %bitcast.9, pred[2,1024]{1,0:T(4,128)(4,1)S(1)} %broadcast_in_dim.14), kind=kOutput, calls=%fused_computation.3 | convolution fusion | flops 2936537088 | bytes 12519424 | tf_op jit(solution)/shard_map/am,oac->omc/dot_general | solution.py:21
  (1 shorter events, 0.0 us)
Async XLA Ops:
  6.5 107.1 %all-gather.3.cloned.1.call-start = ((), (), s32[]{:S(2)}) async-start(), calls=%async_computation | async-start | bytes 17039360 | tf_op jit(solution)/shard_map/all_gather | solution.py:13
  7.3 186.2 %all-gather.5.cloned.1.call-start = ((), (), s32[]{:S(2)}) async-start(), calls=%async_computation.1 | async-start | bytes 5857280 | tf_op jit(solution)/shard_map/all_gather | solution.py:20
Sparse Core Ops, SparseCore 0:
  10.1 103.4 all-gather.2
  116.3 77.0 all-gather.4
where the time goes:
time: 210 us; the launch traced here: 209 us
  waiting for transfers between devices  126 us (60%)
  blocking collectives  42.3 us (20%)
  matrix products  18.5 us (9%)
  between operations  13.4 us (6%)
  local copies, waits for them, and re-layouts  7.51 us (4%)
    all_gather x1, waiting for transfers between devices, body(): lax.all_gather(pair_block, 'rows', axis=0, tiled=True)  104 us
    psum x1, blocking collectives, body(): gathered = lax.psum(partial_sum, 'panel').astype(jnp.bfloat16)  42.3 us
    all_gather x1, waiting for transfers between devices, body(): coef_all = lax.all_gather(virt_coef, 'rows', axis=0, tiled=True)  20.7 us
    dot_general x1, matrix products, body(): jnp.dot(lax.all_gather(pair_block, 'rows', axis=0, tiled=True), resolvent...  9.32 us
    dot_general x1, matrix products, body(): jnp.einsum('am,oac->omc', coef_all, grouped, preferred_element_type=jnp.f...  9.22 us
    gather x1, local copies, waits for them, and re-layouts, body(): grouped = jnp.take(gathered, slot_row, axis=0)  7.5 us
  transfers between devices with their start and end apart: 2, of which 2 were waited for; matrix products, arithmetic and copies ran while one was open for 9% of the time, Pallas kernels for 0%

commit v1 on v0

--- a/solution.py
+++ b/solution.py
@@ -6,11 +6,16 @@
 OCC_B = 2
 
 
+def lead_wires_in(buf, named_axis, dim_at):
+    met_up = jnp.concatenate([buf for _ in range(jax.lax.axis_size(named_axis))], dim_at)
+    return jax.lax.all_to_all(met_up, named_axis, dim_at, dim_at, tiled=True)
+
+
 def body(pair_block, resolvent, virt_coef, slot_row):
     resolvent_round = resolvent.astype(jnp.bfloat16)
     gathered = None
     partial_sum = jnp.dot(
-        lax.all_gather(pair_block, "rows", axis=0, tiled=True),
+        lead_wires_in(pair_block, "rows", dim_at=0),
         resolvent_round,
         preferred_element_type=jnp.float32,
     )

time: 210 us -> 522 us (2.49)
  the two profiles are of different devices: /device:TPU:1 before, /device:TPU:48 now
where the time goes in v1:
time: 522 us; the launch traced here: 520 us
  waiting for transfers between devices  389 us (75%)
  local copies, waits for them, and re-layouts  45 us (9%)
  blocking collectives  42.5 us (8%)
  matrix products  18.6 us (4%)
  between operations  13.8 us (3%)
  starting transfers between devices  11.9 us (2%)
    all_to_all x1, waiting for transfers between devices, lead_wires_in(): return jax.lax.all_to_all(met_up, named_axis, dim_at, dim_at, tiled=True)  388 us
    psum x1, blocking collectives, body(): gathered = lax.psum(partial_sum, 'panel').astype(jnp.bfloat16)  42.5 us
    unnamed x69, local copies, waits for them, and re-layouts  37.4 us
    all_to_all x1, starting transfers between devices, lead_wires_in(): return jax.lax.all_to_all(met_up, named_axis, dim_at, dim_at, tiled=True)  11.9 us
  transfers between devices with their start and end apart: 2, of which 1 were waited for; matrix products, arithmetic and copies ran while one was open for 3% of the time, Pallas kernels for 0%

profile of v1, /device:TPU:48, one launch (start us, length us, event | category | flops | bytes accessed | tf_op | source)
XLA Modules:
  0.0 520.4 jit_solution(12080180762838295572)
XLA Ops:
  6.5 0.0 copy-start
  6.5 1.0 constant_dynamic-update-slice_fusion.63
  7.6 1.0 constant_dynamic-update-slice_fusion.62
  8.6 1.0 constant_dynamic-update-slice_fusion.61
  9.5 1.0 constant_dynamic-update-slice_fusion.60
  10.5 1.0 constant_dynamic-update-slice_fusion.59
  11.5 1.0 constant_dynamic-update-slice_fusion.58
  12.4 1.0 constant_dynamic-update-slice_fusion.57
  13.4 1.0 constant_dynamic-update-slice_fusion.56
  14.4 1.0 constant_dynamic-update-slice_fusion.55
  15.4 1.0 constant_dynamic-update-slice_fusion.54
  16.3 1.0 constant_dynamic-update-slice_fusion.53
  17.3 1.0 constant_dynamic-update-slice_fusion.52
  18.3 1.0 constant_dynamic-update-slice_fusion.51
  19.3 1.0 constant_dynamic-update-slice_fusion.50
  20.2 1.0 constant_dynamic-update-slice_fusion.49
  21.2 1.0 constant_dynamic-update-slice_fusion.48
  22.2 1.0 constant_dynamic-update-slice_fusion.47
  23.1 1.0 constant_dynamic-update-slice_fusion.46
  24.1 1.0 constant_dynamic-update-slice_fusion.45
  25.1 1.0 constant_dynamic-update-slice_fusion.44
  26.1 1.0 constant_dynamic-update-slice_fusion.43
  27.0 1.0 constant_dynamic-update-slice_fusion.42
  28.0 1.0 constant_dynamic-update-slice_fusion.41
  29.0 1.0 constant_dynamic-update-slice_fusion.40
  30.0 1.0 constant_dynamic-update-slice_fusion.39
  30.9 1.0 constant_dynamic-update-slice_fusion.38
  31.9 1.0 constant_dynamic-update-slice_fusion.37
  32.9 1.0 constant_dynamic-update-slice_fusion.36
  33.9 1.0 constant_dynamic-update-slice_fusion.35
  34.8 1.0 constant_dynamic-update-slice_fusion.34
  35.8 1.0 constant_dynamic-update-slice_fusion.33
  36.8 1.0 constant_dynamic-update-slice_fusion.32
  37.7 0.0 copy-done
  38.6 0.0 copy-start.1
  38.6 5.7 %copy-done.1 = bf16[2048,4096]{1,0:T(8,128)(2,1)} copy-done((bf16[2048,4096]{1,0:T(8,128)(2,1)}, bf16[2048,4096]{1,0:T(8,128)(2,1)S(1)}, u32[]{:S(2)}) %copy-start.1) | copy-done | bytes 16777240
  44.4 0.0 copy-start.2
  44.4 11.9 %all-to-all-start = ((bf16[64,32,4096]{2,1,0:T(8,128)(2,1)}), bf16[64,32,4096]{2,1,0:T(8,128)(2,1)}, u32[]{:S(2)}, u32[]{:S(2)}) async-start(bf16[64,32,4096]{2,1,0:T(8,128)(2,1)} %bitcast.11), calls=%async_computation | async-start | bytes 33554432 | tf_op jit(solution)/shard_map/all_to_all | solution.py:11
  56.2 0.0 all-gather.2.cloned.1.call-start
  56.3 0.7 all-gather.2.cloned.1.call-update
  57.0 0.0 copy-done.2
  57.0 387.9 %all-to-all-done = bf16[64,32,4096]{2,1,0:T(8,128)(2,1)} async-done(((bf16[64,32,4096]{2,1,0:T(8,128)(2,1)}), bf16[64,32,4096]{2,1,0:T(8,128)(2,1)}, u32[]{:S(2)}, u32[]{:S(2)}) %all-to-all-start) | async-done | bytes 16777248 | tf_op jit(solution)/shard_map/all_to_all | solution.py:11
  445.0 9.3 %fusion.5 = f32[2048,256]{1,0:T(8,128)S(1)} fusion(bf16[2048,4096]{1,0:T(8,128)(2,1)} %bitcast.1, f32[4096,256]{1,0:T(8,128)} %param.5), kind=kOutput, calls=%fused_computation.4 | convolution fusion | flops 4296015872 | bytes 23068672 | tf_op jit(solution)/shard_map/dot_general | solution.py:17
  454.3 42.5 %all-reduce.1 = bf16[2048,256]{1,0:T(8,128)(2,1)S(1)} all-reduce(f32[2048,256]{1,0:T(8,128)S(1)} %fusion.5), channel_id=1, replica_groups=mesh['rows'=64,'panel'=4] {'panel'}, use_global_device_ids=true, to_apply=%region_0.0 | all-reduce | flops 524288 | bytes 3145728 | tf_op jit(solution)/shard_map/psum | solution.py:22
  496.8 7.5 %gather_fusion = bf16[2048,256]{1,0:T(8,128)(2,1)S(1)} fusion(bf16[2048,256]{1,0:T(8,128)(2,1)S(1)} %all-reduce.1, s32[2048]{0:T(1024)S(1)} %fusion.10), kind=kCustom, calls=%fused_computation | custom fusion | bytes 2105344 | tf_op jit(solution)/shard_map/jit(_take)/gather | solution.py:23
  504.3 0.0 all-gather.2.cloned.1.call-done
  504.3 9.2 %fusion.2 = f32[2,2800,256]{2,1,0:T(8,128)} fusion(bf16[1024,2800]{1,0:T(8,128)(2,1)} %all-gather.2.cloned.1.call-done, bf16[2,1024,256]{2,1,0:T(8,128)(2,1)S(1)} %bitcast.12, pred[2,1024]{1,0:T(4,128)(4,1)S(1)} %broadcast_in_dim.14), kind=kOutput, calls=%fused_computation.3 | convolution fusion | flops 2936537088 | bytes 12519424 | tf_op jit(solution)/shard_map/am,oac->omc/dot_general | solution.py:26
  (35 shorter events, 0.6 us)
Async XLA Ops:
  6.5 31.2 %copy-start = (bf16[32,4096]{1,0:T(8,128)(2,1)S(1)}, bf16[32,4096]{1,0:T(8,128)(2,1)}, u32[]{:S(2)}) copy-start(bf16[32,4096]{1,0:T(8,128)(2,1)} %param.4) | copy-start | bytes 786436
  38.6 5.7 %copy-start.1 = (bf16[2048,4096]{1,0:T(8,128)(2,1)}, bf16[2048,4096]{1,0:T(8,128)(2,1)S(1)}, u32[]{:S(2)}) copy-start(bf16[2048,4096]{1,0:T(8,128)(2,1)S(1)} %constant_dynamic-update-slice_fusion) | copy-start | bytes 50331652
  44.4 12.6 %copy-start.2 = (s32[2048]{0:T(1024)S(1)}, s32[2048]{0:T(1024)}, u32[]{:S(2)}) copy-start(s32[2048]{0:T(1024)} %param.7) | copy-start | bytes 24580
  44.4 400.6 %all-to-all-start = ((bf16[64,32,4096]{2,1,0:T(8,128)(2,1)}), bf16[64,32,4096]{2,1,0:T(8,128)(2,1)}, u32[]{:S(2)}, u32[]{:S(2)}) async-start(bf16[64,32,4096]{2,1,0:T(8,128)(2,1)} %bitcast.11), calls=%async_computation | async-start | bytes 33554432 | tf_op jit(solution)/shard_map/all_to_all | solution.py:11
  56.2 448.1 %all-gather.2.cloned.1.call-start = ((), (), s32[]{:S(2)}) async-start(), calls=%async_computation.1 | async-start | bytes 5857280 | tf_op jit(solution)/shard_map/all_gather | solution.py:25
Sparse Core Ops, SparseCore 0:
  59.8 154.0 all-gather.1
